TPU v7x, 512 devices: a whole 4x8x8 slice. The times are simulated.
512 devices in a mesh: frame: 32 (over y_lo, z, core), space: 16 (over x, y_hi).
Axes of the slice: x: 4, y: 8 (y_hi: 4, y_lo: 2; y = y_hi * 2 + y_lo), z: 8, core: 2. Of those that a mesh axis runs over, the one named last changes fastest.
Arguments:
- spatial_query: bfloat16 [32, 1024, 1152], P('frame', 'space'), may hold values from -24 to 24
- spatial_key: bfloat16 [32, 1024, 1152], P('frame', 'space'), may hold values from -24 to 24
- spatial_value: bfloat16 [32, 1024, 1152], P('frame', 'space'), may hold values from -6 to 6
- latents: bfloat16 [32, 1024, 1152], P('frame', 'space'), may hold values from -6 to 6
- proj_weight: bfloat16 [1152, 1152], P('frame'), may hold values from -0.1875 to 0.1875
- proj_bias: float32 [1152], replicated, may hold values from -3 to 3
- residual_gate: float32 [1152], replicated, may hold values from 0.5 to 1.5
- temporal_shift: float32 [1152], replicated, may hold values from -3 to 3
- temporal_scale: float32 [1152], replicated, may hold values from -0.5 to 0.5
- temporal_weight: bfloat16 [1152, 3456], P('frame'), may hold values from -0.75 to 0.75
- clip_lengths: int32 [16], replicated, may hold values from 1 to 4, 32 in all
Outputs:
- hidden: float32 [32, 1024, 1152], P('frame', 'space')
- temporal_out: float32 [32, 1024, 1152], P('frame', 'space')
Inputs may be any that keep to these rules, and one draw needn't show every extreme that they name: `clip_lengths`: 16 clips fill the 32 frames in order; one clip has exactly 4 frames.
All inputs are finite; a program needn't handle non-finite values.
Results may differ from a plain program's by a relative error of at most 0.012.
Values may be sent and summed in bfloat16 or wider, within the bound.
A program may use at most 64 MiB of HBM per device.

v0:
```python
import math
import jax
import jax.numpy as jnp
from jax import lax
from jax.sharding import Mesh
from jax.sharding import PartitionSpec as P

HEADS = 16
FRAME = ("frame_0", "frame_1", "frame_2")
neg_fill = -1e30


def in_blocks(shard, dim, devices):
    before, after = (shard.shape[:dim], shard.shape[dim + 1 :])
    return jnp.moveaxis(shard.reshape(*before, devices, -1, *after), dim, 0)


def in_order(blocks, dim):
    shape = list(blocks.shape[1:])
    shape[dim] *= blocks.shape[0]
    return jnp.moveaxis(blocks, 0, dim).reshape(shape)


def exchange_in_order(blocks, axes, sequence):
    shape = [lax.axis_size(a) for a in axes]
    blocks = blocks.reshape(*shape, *blocks.shape[1:])
    for k in sequence:
        blocks = lax.all_to_all(blocks, axes[k], split_axis=k, concat_axis=k, tiled=True)
    return blocks.reshape(-1, *blocks.shape[len(axes) :])


def exchange_by_chip(shard, groups, sequence, split_dim, concat_dim):
    devices = lax.axis_size(groups[0]) * lax.axis_size(groups[1])
    blocks = in_blocks(shard, split_dim, devices)
    return in_order(exchange_in_order(blocks, groups, sequence), concat_dim)


def head_scores(query, keys):
    factor = 1.0 / math.sqrt(query.shape[-1])
    return jnp.einsum("fahd,fbhd->fhab", query, keys, preferred_element_type=jnp.float32) * factor


def frame_attention(parts):
    query, keys, values = parts
    frames, count, heads, head_dim = query.shape
    block = math.gcd(count, 512)
    blocks = jnp.moveaxis(query.reshape(frames, count // block, block, heads, head_dim), 1, 0)

    def one_block(rows):
        scores = head_scores(rows, keys)
        top = jnp.max(scores, axis=-1, keepdims=True)
        probs = jnp.exp(scores - top)
        total = jnp.sum(probs, axis=-1)
        mixed = jnp.einsum(
            "fhab,fbhd->fahd",
            probs.astype(jnp.bfloat16),
            values,
            preferred_element_type=jnp.float32,
        )
        return (mixed / jnp.transpose(total, (0, 2, 1))[..., None]).astype(jnp.bfloat16)

    result = lax.map(one_block, blocks)
    return jnp.moveaxis(result, 0, 1).reshape(frames, count, heads, head_dim)


def temporal_mix(packed, allowed):
    frames, count = (packed.shape[0], packed.shape[1])
    width = packed.shape[2] // 3
    head_dim = width // HEADS
    split = (frames, count, HEADS, head_dim)
    query = packed[:, :, :width].reshape(split)
    keys = packed[:, :, width : 2 * width].reshape(split)
    values = packed[:, :, 2 * width :].reshape(split)
    scores = jnp.einsum("anhd,bnhd->nhab", query, keys, preferred_element_type=jnp.float32) * (
        1.0 / math.sqrt(head_dim)
    )
    scores = jnp.where(allowed, scores, neg_fill)
    top = jnp.max(scores, axis=-1, keepdims=True)
    probs = jnp.exp(scores - top)
    total = jnp.sum(probs, axis=-1)
    mixed = jnp.einsum(
        "nhab,bnhd->anhd", probs.astype(jnp.bfloat16), values, preferred_element_type=jnp.float32
    )
    mixed = mixed / jnp.transpose(total, (2, 0, 1))[..., None]
    return mixed.reshape(frames, count, width)


def shards(
    spatial_query,
    spatial_key,
    spatial_value,
    latents,
    proj_weight,
    proj_bias,
    residual_gate,
    temporal_shift,
    temporal_scale,
    temporal_weight,
    clip_lengths,
):
    frames_dev, patches_dev, width = latents.shape
    head_dim = width // HEADS
    split = (frames_dev, patches_dev, HEADS, head_dim)
    query = spatial_query.reshape(split)
    mixed_heads = frame_attention(
        (
            lax.all_to_all(query, "space", split_axis=2, concat_axis=1, tiled=True),
            lax.all_to_all(
                spatial_key.reshape(split), "space", split_axis=2, concat_axis=1, tiled=True
            ),
            lax.all_to_all(
                spatial_value.reshape(split), "space", split_axis=2, concat_axis=1, tiled=True
            ),
        )
    )
    attended = lax.all_to_all(mixed_heads, "space", split_axis=1, concat_axis=2, tiled=True)
    rows = frames_dev * patches_dev
    flat = attended.reshape(rows, width)
    projected = jnp.dot(
        flat,
        lax.all_gather(proj_weight, FRAME, axis=0, tiled=True),
        preferred_element_type=jnp.float32,
    )
    hidden = latents.reshape(rows, width).astype(jnp.float32) + residual_gate * (
        projected + proj_bias
    )
    mean = jnp.mean(hidden, axis=-1, keepdims=True)
    centred = hidden - mean
    variance = jnp.mean(centred * centred, axis=-1, keepdims=True)
    normed = (
        centred * lax.rsqrt(variance + 1e-06) * (1.0 + temporal_scale) + temporal_shift
    ).astype(jnp.bfloat16)
    groups = lax.axis_size(FRAME)
    frames_all = frames_dev * groups
    per_group = patches_dev // groups
    ends = jnp.cumsum(clip_lengths)
    clip_of = jnp.sum(
        (jnp.arange(frames_all, dtype=jnp.int32)[:, None] >= ends[None, :]).astype(jnp.int32),
        axis=1,
    )
    allowed = clip_of[:, None] == clip_of[None, :]
    whole_weight = lax.all_gather(temporal_weight, FRAME, axis=0, tiled=True)
    local = jnp.einsum(
        "fnc,ce->fne",
        exchange_by_chip(
            normed.reshape(frames_dev, groups, per_group, width),
            (("frame_0", "frame_1"), "frame_2"),
            (1, 0),
            1,
            0,
        )[:, 0],
        whole_weight,
        preferred_element_type=jnp.float32,
    ).astype(jnp.bfloat16)
    temporal = temporal_mix(local, allowed)[:, None]
    temporal = temporal.reshape(frames_all, per_group, width)
    temporal_out = lax.all_to_all(
        temporal.astype(jnp.bfloat16), FRAME, split_axis=0, concat_axis=1, tiled=True
    ).astype(temporal.dtype)
    return (hidden.reshape(frames_dev, patches_dev, width), temporal_out)


def solution(mesh):
    split = Mesh(
        mesh.devices.reshape(2, 8, 2, mesh.shape["space"]),
        ("frame_0", "frame_1", "frame_2", "space"),
    )
    return jax.shard_map(
        shards,
        mesh=split,
        in_specs=(
            P(FRAME, "space", None),
            P(FRAME, "space", None),
            P(FRAME, "space", None),
            P(FRAME, "space", None),
            P(FRAME, None),
            P(),
            P(),
            P(),
            P(),
            P(FRAME, None),
            P(),
        ),
        out_specs=(P(FRAME, "space", None), P(FRAME, "space", None)),
        check_vma=False,
    )
```

profile of v0, /device:TPU:1, one launch (start us, length us, event | category | flops | bytes accessed | tf_op | source)
XLA Modules:
  0.0 205.7 jit_solution(14141695110795643575)
XLA Ops:
  7.2 0.7 all-gather.5.cloned.1.call-update
  8.0 0.7 all-gather.7.cloned.1.call-update
  8.7 1.4 reshape.123
  10.0 0.8 copy.88
  10.8 10.2 %all-to-all-start = ((bf16[1,64,16,72]{3,1,0,2:T(8,128)(2,1)}), bf16[1,64,16,72]{3,1,0,2:T(8,128)(2,1)S(1)}, u32[]{:S(2)}, u32[]{:S(2)}) async-start(bf16[1,64,16,72]{3,1,0,2:T(8,128)(2,1)} %copy.88), calls=%async_computation | async-start | bytes 524288 | tf_op jit(solution)/shard_map/all_to_all | solution.py:107
  21.0 1.4 reshape.124
  22.4 0.8 copy.90
  23.2 10.2 %all-to-all-done = bf16[1,64,16,72]{3,1,0,2:T(8,128)(2,1)S(1)} async-done(((bf16[1,64,16,72]{3,1,0,2:T(8,128)(2,1)}), bf16[1,64,16,72]{3,1,0,2:T(8,128)(2,1)S(1)}, u32[]{:S(2)}, u32[]{:S(2)}) %all-to-all-start) | async-done | bytes 147488 | tf_op jit(solution)/shard_map/all_to_all | solution.py:107
  33.4 3.9 %all-to-all-start.1 = ((bf16[1,64,16,72]{3,1,0,2:T(8,128)(2,1)}), bf16[1,64,16,72]{3,1,0,2:T(8,128)(2,1)S(1)}, u32[]{:S(2)}, u32[]{:S(2)}) async-start(bf16[1,64,16,72]{3,1,0,2:T(8,128)(2,1)} %copy.90), calls=%async_computation.1 | async-start | bytes 524288 | tf_op jit(solution)/shard_map/all_to_all | solution.py:108
  37.7 0.8 copy.92
  38.5 13.1 %all-to-all-done.1 = bf16[1,64,16,72]{3,1,0,2:T(8,128)(2,1)S(1)} async-done(((bf16[1,64,16,72]{3,1,0,2:T(8,128)(2,1)}), bf16[1,64,16,72]{3,1,0,2:T(8,128)(2,1)S(1)}, u32[]{:S(2)}, u32[]{:S(2)}) %all-to-all-start.1) | async-done | bytes 147488 | tf_op jit(solution)/shard_map/all_to_all | solution.py:108
  51.6 3.5 %all-to-all-start.2 = ((bf16[1,64,16,72]{3,1,0,2:T(8,128)(2,1)}), bf16[1,64,16,72]{3,1,0,2:T(8,128)(2,1)S(1)}, u32[]{:S(2)}, u32[]{:S(2)}) async-start(bf16[1,64,16,72]{3,1,0,2:T(8,128)(2,1)} %copy.92), calls=%async_computation.2 | async-start | bytes 524288 | tf_op jit(solution)/shard_map/all_to_all | solution.py:111
  55.4 14.1 %all-to-all-done.2 = bf16[1,64,16,72]{3,1,0,2:T(8,128)(2,1)S(1)} async-done(((bf16[1,64,16,72]{3,1,0,2:T(8,128)(2,1)}), bf16[1,64,16,72]{3,1,0,2:T(8,128)(2,1)S(1)}, u32[]{:S(2)}, u32[]{:S(2)}) %all-to-all-start.2) | async-done | bytes 147488 | tf_op jit(solution)/shard_map/all_to_all | solution.py:111
  69.7 3.4 %while.10 = (s32[]{:T(128)}, bf16[2,1,512,1,72]{2,4,3,1,0:T(8,128)(2,1)S(1)}, bf16[2,1,512,1,72]{2,4,3,1,0:T(8,128)(2,1)S(1)}, bf16[1,1024,1,72]{1,3,2,0:T(8,128...) while((s32[]{:T(128)}, bf16[2,1,512,1,72]{2,4,3,1,0:T(8,128)(2,1)S(1)}, ...), condition=%wide.region_3.4_spmd, body=%wide.region_0.3_spmd.sunk | while | flops 155261952 | bytes 6744149 | solution.py:62
  69.7 0.6 multiply_reduce_fusion.3
  70.8 0.6 fusion.40
  72.5 0.6 fusion.40
  73.9 2.3 %reduce.5 = bf16[1024,72]{1,0:T(8,128)(2,1)S(1)} reduce(bf16[1024,1,1,72]{3,2,1,0:T(2,128)(2,1)S(1)} %bitcast.98, bf16[]{:T(256)} %broadcast.46), dimensions={1,2}, to_apply=%bitcast.78.reduce_sub_computation | reduce | bytes 294914
  76.2 1.2 reshape.144
  77.4 3.5 %all-to-all-start.3 = ((bf16[16,2,2304]{2,1,0:T(2,128)(2,1)}), bf16[16,2,2304]{2,1,0:T(2,128)(2,1)S(1)}, u32[]{:S(2)}, u32[]{:S(2)}) async-start(bf16[16,2,2304]{2,1,0:T(2,128)(2,1)} %reshape.144), calls=%async_computation.3 | async-start | bytes 294912 | tf_op jit(solution)/shard_map/all_to_all | solution.py:116
  81.2 9.5 %all-to-all-done.3 = bf16[16,2,2304]{2,1,0:T(2,128)(2,1)S(1)} async-done(((bf16[16,2,2304]{2,1,0:T(2,128)(2,1)}), bf16[16,2,2304]{2,1,0:T(2,128)(2,1)S(1)}, u32[]{:S(2)}, u32[]{:S(2)}) %all-to-all-start.3) | async-done | bytes 147488 | tf_op jit(solution)/shard_map/all_to_all | solution.py:116
  90.7 0.9 reshape.145
  92.9 3.6 %reshape.136 = bf16[1152,1152]{1,0:T(8,128)(2,1)S(1)} reshape(bf16[32,36,1152]{2,1,0:T(8,128)(2,1)} %all-gather.5.cloned.1.call-done) | data formatting | bytes 5308416
  96.6 0.7 fusion.28
  97.8 6.7 %all_to_all.85 = bf16[16,2,1,1,2,1152]{5,4,0,3,2,1:T(2,128)(2,1)S(1)} all-to-all(bf16[16,2,1,1,2,1152]{5,4,0,3,2,1:T(2,128)(2,1)S(1)} %copy.99), channel_id=1, replica_groups=mesh['frame_0'=2,'frame_1'=8,'frame_2'=2,'space'=16] {'frame_2'}, dimensions={1} | all-to-all | bytes 294912 | tf_op jit(solution)/shard_map/all_to_all | solution.py:28
  104.5 0.8 copy.100
  105.3 9.1 %all-to-all-start.5 = ((bf16[16,2,1,1,2,1152]{5,4,1,3,2,0:T(2,128)(2,1)}), bf16[16,2,1,1,2,1152]{5,4,1,3,2,0:T(2,128)(2,1)S(1)}, u32[]{:S(2)}, u32[]{:S(2)}) async-start(bf16[16,2,1,1,2,1152]{5,4,1,3,2,0:T(2,128)(2,1)} %copy.100), calls=%async_computation.5 | async-start | bytes 294912 | tf_op jit(solution)/shard_map/all_to_all | solution.py:28
  114.6 49.2 %all-gather.7.cloned.1.call-done = bf16[32,36,3456]{2,1,0:T(8,128)(2,1)} async-done(((bf16[1,36,3456]{2,1,0:T(8,128)(2,1)}), bf16[32,36,3456]{2,1,0:T(8,128)(2,1)}) %all-gather.7.cloned.1.call-update) | async-done | bytes 7962640 | tf_op jit(solution)/shard_map/all_gather | solution.py:142
  163.8 12.4 %reshape.139 = bf16[1152,3456,1]{1,0,2:T(8,128)(2,1)} reshape(bf16[32,36,3456]{2,1,0:T(8,128)(2,1)} %all-gather.7.cloned.1.call-done) | data formatting | bytes 15925248
  176.2 4.6 %convolution_convert_fusion = bf16[32,2,3456]{2,0,1:T(8,128)(2,1)S(1)} fusion(bf16[1152,3456,1]{1,0,2:T(8,128)(2,1)} %reshape.139, bf16[32,2,1152]{2,1,0:T(2,128)(2,1)S(1)} %bitcast.104), kind=kOutput, calls=%fused_computation.16 | convolution fusion | flops 509829120 | bytes 8552448 | tf_op jit(solution)/shard_map/fnc,ce->fne/dot_general | solution.py:143
  183.5 14.6 %all_to_all.86 = bf16[32,2,1152]{2,1,0:T(2,128)(2,1)S(1)} all-to-all(bf16[32,2,1152]{2,1,0:T(2,128)(2,1)S(1)} %reshape.142), channel_id=1, replica_groups=mesh['frame_0'=2,'frame_1'=8,'frame_2'=2,'space'=16] {'frame_0','frame_1..., dimensions={0} | all-to-all | bytes 294912 | tf_op jit(solution)/shard_map/all_to_all | solution.py:157
  198.1 0.8 reshape.134
  (56 shorter events, 8.2 us)
Async XLA Ops:
  7.2 30.1 %copy-start.1 = (bf16[1,64,1152]{2,1,0:T(8,128)(2,1)S(1)}, bf16[1,64,1152]{2,1,0:T(8,128)(2,1)}, u32[]{:S(2)}) copy-start(bf16[1,64,1152]{2,1,0:T(8,128)(2,1)} %param.15) | copy-start | bytes 442372
  7.2 85.7 %all-gather.5.cloned.1.call-start = ((), (), s32[]{:S(2)}) async-start(), calls=%async_computation.7 | async-start | bytes 3041280 | tf_op jit(solution)/shard_map/all_gather | solution.py:121
  7.9 155.8 %all-gather.7.cloned.1.call-start = ((), (), s32[]{:S(2)}) async-start(), calls=%async_computation.8 | async-start | bytes 9123840 | tf_op jit(solution)/shard_map/all_gather | solution.py:142
  10.8 22.6 %all-to-all-start = ((bf16[1,64,16,72]{3,1,0,2:T(8,128)(2,1)}), bf16[1,64,16,72]{3,1,0,2:T(8,128)(2,1)S(1)}, u32[]{:S(2)}, u32[]{:S(2)}) async-start(bf16[1,64,16,72]{3,1,0,2:T(8,128)(2,1)} %copy.88), calls=%async_computation | async-start | bytes 524288 | tf_op jit(solution)/shard_map/all_to_all | solution.py:107
  33.4 18.2 %all-to-all-start.1 = ((bf16[1,64,16,72]{3,1,0,2:T(8,128)(2,1)}), bf16[1,64,16,72]{3,1,0,2:T(8,128)(2,1)S(1)}, u32[]{:S(2)}, u32[]{:S(2)}) async-start(bf16[1,64,16,72]{3,1,0,2:T(8,128)(2,1)} %copy.90), calls=%async_computation.1 | async-start | bytes 524288 | tf_op jit(solution)/shard_map/all_to_all | solution.py:108
  51.6 18.0 %all-to-all-start.2 = ((bf16[1,64,16,72]{3,1,0,2:T(8,128)(2,1)}), bf16[1,64,16,72]{3,1,0,2:T(8,128)(2,1)S(1)}, u32[]{:S(2)}, u32[]{:S(2)}) async-start(bf16[1,64,16,72]{3,1,0,2:T(8,128)(2,1)} %copy.92), calls=%async_computation.2 | async-start | bytes 524288 | tf_op jit(solution)/shard_map/all_to_all | solution.py:111
  73.1 7.8 %copy-start.7 = (s32[16]{0:T(128)S(1)}, s32[16]{0:T(128)}, u32[]{:S(2)}) copy-start(s32[16]{0:T(128)} %param.23) | copy-start | bytes 196
  73.1 8.1 %copy-start.6 = (f32[1152]{0:T(1024)S(1)}, f32[1152]{0:T(1024)}, u32[]{:S(2)}) copy-start(f32[1152]{0:T(1024)} %param.21) | copy-start | bytes 13828
  77.4 13.3 %all-to-all-start.3 = ((bf16[16,2,2304]{2,1,0:T(2,128)(2,1)}), bf16[16,2,2304]{2,1,0:T(2,128)(2,1)S(1)}, u32[]{:S(2)}, u32[]{:S(2)}) async-start(bf16[16,2,2304]{2,1,0:T(2,128)(2,1)} %reshape.144), calls=%async_computation.3 | async-start | bytes 294912 | tf_op jit(solution)/shard_map/all_to_all | solution.py:116
  92.8 3.7 %copy-start.2 = (bf16[1,64,1152]{2,1,0:T(8,128)(2,1)S(1)}, bf16[1,64,1152]{2,1,0:T(8,128)(2,1)}, u32[]{:S(2)}) copy-start(bf16[1,64,1152]{2,1,0:T(8,128)(2,1)} %param.16) | copy-start | bytes 442372
  92.9 3.7 %copy-start.3 = (f32[1152]{0:T(1024)S(1)}, f32[1152]{0:T(1024)}, u32[]{:S(2)}) copy-start(f32[1152]{0:T(1024)} %param.18) | copy-start | bytes 13828
  92.9 3.7 %copy-start.4 = (f32[1152]{0:T(1024)S(1)}, f32[1152]{0:T(1024)}, u32[]{:S(2)}) copy-start(f32[1152]{0:T(1024)} %param.19) | copy-start | bytes 13828
  96.6 0.9 copy-start.5
  97.3 78.9 %copy-start = (f32[64,1152]{1,0:T(8,128)}, f32[64,1152]{1,0:T(8,128)S(1)}, u32[]{:S(2)}) copy-start(f32[64,1152]{1,0:T(8,128)S(1)} %get-tuple-element.71) | copy-start | bytes 884740
  105.3 70.9 %all-to-all-start.5 = ((bf16[16,2,1,1,2,1152]{5,4,1,3,2,0:T(2,128)(2,1)}), bf16[16,2,1,1,2,1152]{5,4,1,3,2,0:T(2,128)(2,1)S(1)}, u32[]{:S(2)}, u32[]{:S(2)}) async-start(bf16[16,2,1,1,2,1152]{5,4,1,3,2,0:T(2,128)(2,1)} %copy.100), calls=%async_computation.5 | async-start | bytes 294912 | tf_op jit(solution)/shard_map/all_to_all | solution.py:28
Sparse Core Ops, SparseCore 0:
  10.1 74.3 all-gather.4
  86.6 77.0 all-gather.6
where the time goes:
time: 207 us; the launch traced here: 206 us
  waiting for transfers between devices  97.6 us (47%)
  starting transfers between devices  30.3 us (15%)
  local copies, waits for them, and re-layouts  29.8 us (14%)
  blocking collectives  21.3 us (10%)
  between operations  14.4 us (7%)
  matrix products  8.13 us (4%)
  other arithmetic  4.11 us (2%)
    all_gather x1, waiting for transfers between devices, shards(): whole_weight = lax.all_gather(temporal_weight, FRAME, axis=0, tiled=True)  49.2 us
    unnamed x21, local copies, waits for them, and re-layouts  18.7 us
    all_to_all x1, blocking collectives, shards(): lax.all_to_all(temporal.astype(jnp.bfloat16), FRAME, split_axis=0, concat...  14.6 us
    all_to_all x1, waiting for transfers between devices, shards(): lax.all_to_all(spatial_value.reshape(split), 'space', split_axis=2, conca...  14.1 us
    all_to_all x1, waiting for transfers between devices, shards(): lax.all_to_all(spatial_key.reshape(split), 'space', split_axis=2, concat_...  13.1 us
    all_to_all x1, starting transfers between devices, shards(): lax.all_to_all(query, 'space', split_axis=2, concat_axis=1, tiled=True)  10.2 us
    all_to_all x1, waiting for transfers between devices, shards(): lax.all_to_all(query, 'space', split_axis=2, concat_axis=1, tiled=True)  10.2 us
    all_to_all x1, waiting for transfers between devices, shards(): lax.all_to_all(mixed_heads, 'space', split_axis=1, concat_axis=2, tiled=T...  9.53 us
  transfers between devices with their start and end apart: 7, of which 5 were waited for; matrix products, arithmetic and copies ran while one was open for 16% of the time, Pallas kernels for 0%

commit v1 on v0

--- a/solution.py
+++ b/solution.py
@@ -154,8 +154,14 @@
     ).astype(jnp.bfloat16)
     temporal = temporal_mix(local, allowed)[:, None]
     temporal = temporal.reshape(frames_all, per_group, width)
-    temporal_out = lax.all_to_all(
-        temporal.astype(jnp.bfloat16), FRAME, split_axis=0, concat_axis=1, tiled=True
+    temporal_out = jnp.concatenate(
+        lax.all_to_all(
+            jnp.stack(jnp.split(temporal.astype(jnp.bfloat16), lax.axis_size(FRAME), axis=0)),
+            FRAME,
+            0,
+            0,
+        ),
+        axis=1,
     ).astype(temporal.dtype)
     return (hidden.reshape(frames_dev, patches_dev, width), temporal_out)
 

time: 207 us -> 212 us (1.024)
  local copies, waits for them, and re-layouts: 29.8 us -> 34.3 us
    another operation x1 -> x34, local copies, waits for them, and re-layouts: 0.08 us -> 3.16 us  [the longest x33 3.08 us: shards(): jnp.stack(jnp.split(temporal.astype(jnp.bfloat16), lax.axis_size(FRAME),...]
    unnamed x21 -> x52, local copies, waits for them, and re-layouts: 18.7 us -> 19.1 us
where the time goes in v1:
time: 212 us; the launch traced here: 211 us
  waiting for transfers between devices  97.6 us (46%)
  local copies, waits for them, and re-layouts  34.3 us (16%)
  starting transfers between devices  30.3 us (14%)
  blocking collectives  21.3 us (10%)
  between operations  14.7 us (7%)
  matrix products  8.13 us (4%)
  other arithmetic  4.11 us (2%)
    all_gather x1, waiting for transfers between devices, shards(): whole_weight = lax.all_gather(temporal_weight, FRAME, axis=0, tiled=True)  49.2 us
    unnamed x52, local copies, waits for them, and re-layouts  19.1 us
    all_to_all x1, blocking collectives, shards(): lax.all_to_all(jnp.stack(jnp.split(temporal.astype(jnp.bfloat16), lax.axi...  14.6 us
    all_to_all x1, waiting for transfers between devices, shards(): lax.all_to_all(spatial_value.reshape(split), 'space', split_axis=2, conca...  14.1 us
    all_to_all x1, waiting for transfers between devices, shards(): lax.all_to_all(spatial_key.reshape(split), 'space', split_axis=2, concat_...  13.1 us
    all_to_all x1, starting transfers between devices, shards(): lax.all_to_all(query, 'space', split_axis=2, concat_axis=1, tiled=True)  10.2 us
    all_to_all x1, waiting for transfers between devices, shards(): lax.all_to_all(query, 'space', split_axis=2, concat_axis=1, tiled=True)  10.2 us
    all_to_all x1, waiting for transfers between devices, shards(): lax.all_to_all(mixed_heads, 'space', split_axis=1, concat_axis=2, tiled=T...  9.53 us
  transfers between devices with their start and end apart: 7, of which 5 were waited for; matrix products, arithmetic and copies ran while one was open for 16% of the time, Pallas kernels for 0%

profile of v1, /device:TPU:1, one launch (start us, length us, event | category | flops | bytes accessed | tf_op | source)
XLA Modules:
  0.0 210.5 jit_solution(3830157419786683748)
XLA Ops:
  7.2 0.7 all-gather.5.cloned.1.call-update
  8.0 0.7 all-gather.7.cloned.1.call-update
  8.7 1.4 reshape.185
  10.0 0.8 copy.69
  10.8 10.2 %all-to-all-start = ((bf16[1,64,16,72]{3,1,0,2:T(8,128)(2,1)}), bf16[1,64,16,72]{3,1,0,2:T(8,128)(2,1)S(1)}, u32[]{:S(2)}, u32[]{:S(2)}) async-start(bf16[1,64,16,72]{3,1,0,2:T(8,128)(2,1)} %copy.69), calls=%async_computation | async-start | bytes 524288 | tf_op jit(solution)/shard_map/all_to_all | solution.py:107
  21.0 1.4 reshape.186
  22.4 0.8 copy.71
  23.2 10.2 %all-to-all-done = bf16[1,64,16,72]{3,1,0,2:T(8,128)(2,1)S(1)} async-done(((bf16[1,64,16,72]{3,1,0,2:T(8,128)(2,1)}), bf16[1,64,16,72]{3,1,0,2:T(8,128)(2,1)S(1)}, u32[]{:S(2)}, u32[]{:S(2)}) %all-to-all-start) | async-done | bytes 147488 | tf_op jit(solution)/shard_map/all_to_all | solution.py:107
  33.4 3.9 %all-to-all-start.1 = ((bf16[1,64,16,72]{3,1,0,2:T(8,128)(2,1)}), bf16[1,64,16,72]{3,1,0,2:T(8,128)(2,1)S(1)}, u32[]{:S(2)}, u32[]{:S(2)}) async-start(bf16[1,64,16,72]{3,1,0,2:T(8,128)(2,1)} %copy.71), calls=%async_computation.1 | async-start | bytes 524288 | tf_op jit(solution)/shard_map/all_to_all | solution.py:108
  37.7 0.8 copy.73
  38.5 13.1 %all-to-all-done.1 = bf16[1,64,16,72]{3,1,0,2:T(8,128)(2,1)S(1)} async-done(((bf16[1,64,16,72]{3,1,0,2:T(8,128)(2,1)}), bf16[1,64,16,72]{3,1,0,2:T(8,128)(2,1)S(1)}, u32[]{:S(2)}, u32[]{:S(2)}) %all-to-all-start.1) | async-done | bytes 147488 | tf_op jit(solution)/shard_map/all_to_all | solution.py:108
  51.6 3.5 %all-to-all-start.2 = ((bf16[1,64,16,72]{3,1,0,2:T(8,128)(2,1)}), bf16[1,64,16,72]{3,1,0,2:T(8,128)(2,1)S(1)}, u32[]{:S(2)}, u32[]{:S(2)}) async-start(bf16[1,64,16,72]{3,1,0,2:T(8,128)(2,1)} %copy.73), calls=%async_computation.2 | async-start | bytes 524288 | tf_op jit(solution)/shard_map/all_to_all | solution.py:111
  55.4 14.1 %all-to-all-done.2 = bf16[1,64,16,72]{3,1,0,2:T(8,128)(2,1)S(1)} async-done(((bf16[1,64,16,72]{3,1,0,2:T(8,128)(2,1)}), bf16[1,64,16,72]{3,1,0,2:T(8,128)(2,1)S(1)}, u32[]{:S(2)}, u32[]{:S(2)}) %all-to-all-start.2) | async-done | bytes 147488 | tf_op jit(solution)/shard_map/all_to_all | solution.py:111
  69.7 3.4 %while.10 = (s32[]{:T(128)}, bf16[2,1,512,1,72]{2,4,3,1,0:T(8,128)(2,1)S(1)}, bf16[2,1,512,1,72]{2,4,3,1,0:T(8,128)(2,1)S(1)}, bf16[1,1024,1,72]{1,3,2,0:T(8,128...) while((s32[]{:T(128)}, bf16[2,1,512,1,72]{2,4,3,1,0:T(8,128)(2,1)S(1)}, ...), condition=%wide.region_3.4_spmd, body=%wide.region_0.3_spmd.sunk | while | flops 155261952 | bytes 6744149 | solution.py:62
  70.8 0.6 fusion.40
  73.9 2.3 %reduce.69 = bf16[1024,72]{1,0:T(8,128)(2,1)S(1)} reduce(bf16[1024,1,1,72]{3,2,1,0:T(2,128)(2,1)S(1)} %bitcast.96, bf16[]{:T(256)} %broadcast.78), dimensions={1,2}, to_apply=%bitcast.76.reduce_sub_computation | reduce | bytes 294914
  76.2 1.2 reshape.237
  77.4 3.5 %all-to-all-start.3 = ((bf16[16,2,2304]{2,1,0:T(2,128)(2,1)}), bf16[16,2,2304]{2,1,0:T(2,128)(2,1)S(1)}, u32[]{:S(2)}, u32[]{:S(2)}) async-start(bf16[16,2,2304]{2,1,0:T(2,128)(2,1)} %reshape.237), calls=%async_computation.3 | async-start | bytes 294912 | tf_op jit(solution)/shard_map/all_to_all | solution.py:116
  81.2 9.5 %all-to-all-done.3 = bf16[16,2,2304]{2,1,0:T(2,128)(2,1)S(1)} async-done(((bf16[16,2,2304]{2,1,0:T(2,128)(2,1)}), bf16[16,2,2304]{2,1,0:T(2,128)(2,1)S(1)}, u32[]{:S(2)}, u32[]{:S(2)}) %all-to-all-start.3) | async-done | bytes 147488 | tf_op jit(solution)/shard_map/all_to_all | solution.py:116
  90.7 0.9 reshape.238
  92.9 3.6 %reshape.198 = bf16[1152,1152]{1,0:T(8,128)(2,1)S(1)} reshape(bf16[32,36,1152]{2,1,0:T(8,128)(2,1)} %all-gather.5.cloned.1.call-done) | data formatting | bytes 5308416
  96.6 0.7 fusion.28
  97.8 6.7 %all_to_all.81 = bf16[16,2,1,1,2,1152]{5,4,0,3,2,1:T(2,128)(2,1)S(1)} all-to-all(bf16[16,2,1,1,2,1152]{5,4,0,3,2,1:T(2,128)(2,1)S(1)} %copy.80), channel_id=1, replica_groups=mesh['frame_0'=2,'frame_1'=8,'frame_2'=2,'space'=16] {'frame_2'}, dimensions={1} | all-to-all | bytes 294912 | tf_op jit(solution)/shard_map/all_to_all | solution.py:28
  104.5 0.8 copy.81
  105.3 9.1 %all-to-all-start.5 = ((bf16[16,2,1,1,2,1152]{5,4,1,3,2,0:T(2,128)(2,1)}), bf16[16,2,1,1,2,1152]{5,4,1,3,2,0:T(2,128)(2,1)S(1)}, u32[]{:S(2)}, u32[]{:S(2)}) async-start(bf16[16,2,1,1,2,1152]{5,4,1,3,2,0:T(2,128)(2,1)} %copy.81), calls=%async_computation.5 | async-start | bytes 294912 | tf_op jit(solution)/shard_map/all_to_all | solution.py:28
  114.6 49.2 %all-gather.7.cloned.1.call-done = bf16[32,36,3456]{2,1,0:T(8,128)(2,1)} async-done(((bf16[1,36,3456]{2,1,0:T(8,128)(2,1)}), bf16[32,36,3456]{2,1,0:T(8,128)(2,1)}) %all-gather.7.cloned.1.call-update) | async-done | bytes 7962640 | tf_op jit(solution)/shard_map/all_gather | solution.py:142
  163.8 12.4 %reshape.201 = bf16[1152,3456,1]{1,0,2:T(8,128)(2,1)} reshape(bf16[32,36,3456]{2,1,0:T(8,128)(2,1)} %all-gather.7.cloned.1.call-done) | data formatting | bytes 15925248
  176.2 4.6 %convolution_convert_fusion = bf16[32,2,3456]{2,0,1:T(8,128)(2,1)S(1)} fusion(bf16[1152,3456,1]{1,0,2:T(8,128)(2,1)} %reshape.201, bf16[32,2,1152]{2,1,0:T(2,128)(2,1)S(1)} %bitcast.102), kind=kOutput, calls=%fused_computation.16 | convolution fusion | flops 509829120 | bytes 8552448 | tf_op jit(solution)/shard_map/fnc,ce->fne/dot_general | solution.py:143
  183.0 0.6 slice_reduce_fusion.19
  183.6 0.9 slice_reduce_fusion
  188.3 14.6 %all_to_all.82 = bf16[32,1,2,1152]{3,2,1,0:T(2,128)(2,1)S(1)} all-to-all(bf16[32,1,2,1152]{3,2,1,0:T(2,128)(2,1)S(1)} %constant_dynamic-update-slice_fusion), channel_id=1, replica_groups=mesh['frame_0'=2,'frame_1'=8,'frame_2'=2,'space'=16] {'frame_0','frame_1..., dimensions={0} | all-to-all | bytes 294912 | tf_op jit(solution)/shard_map/all_to_all | solution.py:158
  202.9 0.8 reshape.196
  (120 shorter events, 12.3 us)
Async XLA Ops:
  7.2 30.1 %copy-start.1 = (bf16[1,64,1152]{2,1,0:T(8,128)(2,1)S(1)}, bf16[1,64,1152]{2,1,0:T(8,128)(2,1)}, u32[]{:S(2)}) copy-start(bf16[1,64,1152]{2,1,0:T(8,128)(2,1)} %param.15) | copy-start | bytes 442372
  7.2 85.7 %all-gather.5.cloned.1.call-start = ((), (), s32[]{:S(2)}) async-start(), calls=%async_computation.7 | async-start | bytes 3041280 | tf_op jit(solution)/shard_map/all_gather | solution.py:121
  7.9 155.8 %all-gather.7.cloned.1.call-start = ((), (), s32[]{:S(2)}) async-start(), calls=%async_computation.8 | async-start | bytes 9123840 | tf_op jit(solution)/shard_map/all_gather | solution.py:142
  10.8 22.6 %all-to-all-start = ((bf16[1,64,16,72]{3,1,0,2:T(8,128)(2,1)}), bf16[1,64,16,72]{3,1,0,2:T(8,128)(2,1)S(1)}, u32[]{:S(2)}, u32[]{:S(2)}) async-start(bf16[1,64,16,72]{3,1,0,2:T(8,128)(2,1)} %copy.69), calls=%async_computation | async-start | bytes 524288 | tf_op jit(solution)/shard_map/all_to_all | solution.py:107
  33.4 18.2 %all-to-all-start.1 = ((bf16[1,64,16,72]{3,1,0,2:T(8,128)(2,1)}), bf16[1,64,16,72]{3,1,0,2:T(8,128)(2,1)S(1)}, u32[]{:S(2)}, u32[]{:S(2)}) async-start(bf16[1,64,16,72]{3,1,0,2:T(8,128)(2,1)} %copy.71), calls=%async_computation.1 | async-start | bytes 524288 | tf_op jit(solution)/shard_map/all_to_all | solution.py:108
  51.6 18.0 %all-to-all-start.2 = ((bf16[1,64,16,72]{3,1,0,2:T(8,128)(2,1)}), bf16[1,64,16,72]{3,1,0,2:T(8,128)(2,1)S(1)}, u32[]{:S(2)}, u32[]{:S(2)}) async-start(bf16[1,64,16,72]{3,1,0,2:T(8,128)(2,1)} %copy.73), calls=%async_computation.2 | async-start | bytes 524288 | tf_op jit(solution)/shard_map/all_to_all | solution.py:111
  73.1 7.8 %copy-start.7 = (s32[16]{0:T(128)S(1)}, s32[16]{0:T(128)}, u32[]{:S(2)}) copy-start(s32[16]{0:T(128)} %param.23) | copy-start | bytes 196
  73.1 8.1 %copy-start.6 = (f32[1152]{0:T(1024)S(1)}, f32[1152]{0:T(1024)}, u32[]{:S(2)}) copy-start(f32[1152]{0:T(1024)} %param.21) | copy-start | bytes 13828
  77.4 13.3 %all-to-all-start.3 = ((bf16[16,2,2304]{2,1,0:T(2,128)(2,1)}), bf16[16,2,2304]{2,1,0:T(2,128)(2,1)S(1)}, u32[]{:S(2)}, u32[]{:S(2)}) async-start(bf16[16,2,2304]{2,1,0:T(2,128)(2,1)} %reshape.237), calls=%async_computation.3 | async-start | bytes 294912 | tf_op jit(solution)/shard_map/all_to_all | solution.py:116
  92.8 3.7 %copy-start.2 = (bf16[1,64,1152]{2,1,0:T(8,128)(2,1)S(1)}, bf16[1,64,1152]{2,1,0:T(8,128)(2,1)}, u32[]{:S(2)}) copy-start(bf16[1,64,1152]{2,1,0:T(8,128)(2,1)} %param.16) | copy-start | bytes 442372
  92.9 3.7 %copy-start.3 = (f32[1152]{0:T(1024)S(1)}, f32[1152]{0:T(1024)}, u32[]{:S(2)}) copy-start(f32[1152]{0:T(1024)} %param.18) | copy-start | bytes 13828
  92.9 3.7 %copy-start.4 = (f32[1152]{0:T(1024)S(1)}, f32[1152]{0:T(1024)}, u32[]{:S(2)}) copy-start(f32[1152]{0:T(1024)} %param.19) | copy-start | bytes 13828
  96.6 0.9 copy-start.5
  97.3 78.9 %copy-start = (f32[64,1152]{1,0:T(8,128)}, f32[64,1152]{1,0:T(8,128)S(1)}, u32[]{:S(2)}) copy-start(f32[64,1152]{1,0:T(8,128)S(1)} %get-tuple-element.98) | copy-start | bytes 884740
  105.3 70.9 %all-to-all-start.5 = ((bf16[16,2,1,1,2,1152]{5,4,1,3,2,0:T(2,128)(2,1)}), bf16[16,2,1,1,2,1152]{5,4,1,3,2,0:T(2,128)(2,1)S(1)}, u32[]{:S(2)}, u32[]{:S(2)}) async-start(bf16[16,2,1,1,2,1152]{5,4,1,3,2,0:T(2,128)(2,1)} %copy.81), calls=%async_computation.5 | async-start | bytes 294912 | tf_op jit(solution)/shard_map/all_to_all | solution.py:28
Sparse Core Ops, SparseCore 0:
  10.1 74.3 all-gather.4
  86.6 77.0 all-gather.6
